TPU v7x, 32 devices: a whole 2x2x4 slice. The times are simulated.
32 devices in a mesh: dp: 4 (over x, core), pipe: 2 (over y), tensor: 4 (over z).
Axes of the slice: x: 2, y: 2, z: 4, core: 2. Of those that a mesh axis runs over, the one named last changes fastest.
Arguments:
- weights: bfloat16 [2816, 1408], P(('dp', 'pipe', 'tensor')), may hold values from -6 to 6
- first_moment: bfloat16 [2816, 1408], P(('dp', 'pipe', 'tensor')), may hold values from -6 to 6
- second_moment: bfloat16 [2816, 1408], P(('dp', 'pipe', 'tensor')), may hold values from 0.049804688 to 5
- row_weight: float32 [1408], replicated, may hold values from -1 to 1
- col_weight: float32 [1408], replicated, may hold values from 1 to 4
Outputs:
- weight_tiles: bfloat16 [2816, 1408], P(('pipe', 'tensor'))
- first_tiles: bfloat16 [2816, 1408], P(('pipe', 'tensor'))
- second_tiles: bfloat16 [2816, 1408], P(('pipe', 'tensor'))
- checksums: float32 [3, 2, 4, 11], P(None, 'pipe', 'tensor')
All inputs are finite; a program needn't handle non-finite values.
Results may differ from a plain program's by a relative error of at most 0.001.
Values may be sent and summed in bfloat16 or wider, within the bound.
A program may use at most 64 MiB of HBM per device.

v0:
```python
import jax
import jax.numpy as jnp
from jax import lax
from jax.sharding import PartitionSpec as P

CHECK_COLS = 128


def for_sending(array):
    return jax.tree.map(lambda a: a.astype(jnp.bfloat16) if a.dtype == jnp.float32 else a, array)


def column_sums(data, row_part, col_weight, col_blocks):
    row_mixed = jnp.dot(
        row_part[None, :], data.astype(jnp.float32), precision=lax.Precision.HIGHEST
    )[0]
    return jnp.sum((row_mixed * col_weight).reshape(col_blocks, -1), axis=1)


def shards(weights, first_moment, second_moment, row_weight, col_weight):
    dp_count = lax.axis_size("dp")
    pipe_count = lax.axis_size("pipe")
    tensor_count = lax.axis_size("tensor")
    shard_rows, width = weights.shape
    dp_section = dp_count // pipe_count
    tile_shards = dp_count // tensor_count
    piece_cols = width // dp_count
    tile_rows = shard_rows * dp_count
    col_blocks = width // CHECK_COLS
    factor = float(tile_rows * CHECK_COLS) ** (-0.5)
    sources = (weights, first_moment, second_moment)
    exchanged = (
        lax.all_to_all(sources[0], "dp", split_axis=1, concat_axis=0, tiled=True),
        lax.all_to_all(sources[1], "dp", split_axis=1, concat_axis=0, tiled=True),
        lax.all_to_all(sources[2], "dp", split_axis=1, concat_axis=0, tiled=True),
    )
    grouped = tuple(
        (item.reshape(pipe_count, dp_section, shard_rows, piece_cols) for item in exchanged)
    )
    sectioned = jax.tree.map(
        lambda part, own: part.astype(own.dtype),
        lax.all_to_all(for_sending(grouped), "pipe", split_axis=0, concat_axis=2, tiled=True),
        grouped,
    )
    routed = tuple(
        (item.reshape(tensor_count, tile_shards, 1, shard_rows, piece_cols) for item in sectioned)
    )
    arrived = jax.tree.map(
        lambda part, own: part.astype(own.dtype),
        lax.all_to_all(for_sending(routed), "tensor", split_axis=0, concat_axis=2, tiled=True),
        routed,
    )
    flat_pieces = tuple((item.reshape(tile_rows, piece_cols) for item in arrived))
    tiles = jax.tree.map(
        lambda part, own: part.astype(own.dtype),
        lax.all_gather(for_sending(flat_pieces), "dp", axis=1, tiled=True),
        flat_pieces,
    )
    tensor_pos = lax.axis_index("tensor")
    flat_index = (
        lax.axis_index("dp") * pipe_count + lax.axis_index("pipe")
    ) * tensor_count + tensor_pos
    in_section = flat_index % (dp_count * tensor_count)
    section_of = flat_index // (dp_count * tensor_count)
    tile_of = in_section // dp_count
    row_part = lax.dynamic_slice_in_dim(row_weight, in_section * shard_rows, shard_rows)
    partial_value = jnp.stack(
        [column_sums(item, row_part, col_weight, col_blocks) for item in sources]
    )
    section_hit = (jnp.arange(pipe_count) == section_of).astype(jnp.float32)
    tile_hit = (jnp.arange(tensor_count) == tile_of).astype(jnp.float32)
    spread = (
        partial_value[:, None, None, :]
        * section_hit[None, :, None, None]
        * tile_hit[None, None, :, None]
    )
    summed = lax.psum(spread, ("dp", "pipe", "tensor"))
    checks = (
        lax.dynamic_slice(summed, (0, lax.axis_index("pipe"), tensor_pos, 0), (3, 1, 1, col_blocks))
        * factor
    )
    return (tiles[0], tiles[1], tiles[2], checks)


def solution(mesh):
    return jax.shard_map(
        shards,
        mesh=mesh,
        in_specs=(
            P(("dp", "pipe", "tensor"), None),
            P(("dp", "pipe", "tensor"), None),
            P(("dp", "pipe", "tensor"), None),
            P(),
            P(),
        ),
        out_specs=(
            P(("pipe", "tensor"), None),
            P(("pipe", "tensor"), None),
            P(("pipe", "tensor"), None),
            P(None, "pipe", "tensor", None),
        ),
        check_vma=False,
    )
```

profile of v0, /device:TPU:0, one launch (start us, length us, event | category | flops | bytes accessed | tf_op | source)
XLA Modules:
  0.0 154.1 jit_solution(8427268718347811385)
XLA Ops:
  0.6 0.0 copy-start
  0.6 0.0 copy-start.3
  0.7 1.3 all_to_all.90
  1.9 0.7 copy.33
  2.7 4.4 %all-to-all-start = ((bf16[88,4,352]{2,0,1:T(8,128)(2,1)}), bf16[88,4,352]{2,0,1:T(8,128)(2,1)}, u32[]{:S(2)}, u32[]{:S(2)}) async-start(bf16[88,4,352]{2,0,1:T(8,128)(2,1)} %copy.33), calls=%async_computation | async-start | bytes 540672 | tf_op jit(solution)/shard_map/all_to_all | solution.py:33
  7.0 0.0 copy-done.3
  7.0 0.3 all_to_all.97
  7.3 0.7 copy.37
  8.1 5.6 %all-to-all-done = bf16[88,4,352]{2,0,1:T(8,128)(2,1)} async-done(((bf16[88,4,352]{2,0,1:T(8,128)(2,1)}), bf16[88,4,352]{2,0,1:T(8,128)(2,1)}, u32[]{:S(2)}, u32[]{:S(2)}) %all-to-all-start) | async-done | bytes 247840 | tf_op jit(solution)/shard_map/all_to_all | solution.py:33
  13.7 4.1 %all-to-all-start.3 = ((bf16[88,4,352]{2,0,1:T(8,128)(2,1)}), bf16[88,4,352]{2,0,1:T(8,128)(2,1)}, u32[]{:S(2)}, u32[]{:S(2)}) async-start(bf16[88,4,352]{2,0,1:T(8,128)(2,1)} %copy.37), calls=%async_computation.3 | async-start | bytes 540672 | tf_op jit(solution)/shard_map/all_to_all | solution.py:34
  17.8 0.3 all_to_all.104
  18.1 0.0 copy-start.4
  18.1 0.7 copy.41
  18.9 5.1 %all-to-all-done.3 = bf16[88,4,352]{2,0,1:T(8,128)(2,1)} async-done(((bf16[88,4,352]{2,0,1:T(8,128)(2,1)}), bf16[88,4,352]{2,0,1:T(8,128)(2,1)}, u32[]{:S(2)}, u32[]{:S(2)}) %all-to-all-start.3) | async-done | bytes 247840 | tf_op jit(solution)/shard_map/all_to_all | solution.py:34
  24.0 4.1 %all-to-all-start.6 = ((bf16[88,4,352]{2,0,1:T(8,128)(2,1)}), bf16[88,4,352]{2,0,1:T(8,128)(2,1)}, u32[]{:S(2)}, u32[]{:S(2)}) async-start(bf16[88,4,352]{2,0,1:T(8,128)(2,1)} %copy.41), calls=%async_computation.6 | async-start | bytes 540672 | tf_op jit(solution)/shard_map/all_to_all | solution.py:35
  28.1 0.3 convolution_reduce_fusion.2
  28.4 0.3 convolution_reduce_fusion
  28.7 5.5 %all-to-all-done.6 = bf16[88,4,352]{2,0,1:T(8,128)(2,1)} async-done(((bf16[88,4,352]{2,0,1:T(8,128)(2,1)}), bf16[88,4,352]{2,0,1:T(8,128)(2,1)}, u32[]{:S(2)}, u32[]{:S(2)}) %all-to-all-start.6) | async-done | bytes 247840 | tf_op jit(solution)/shard_map/all_to_all | solution.py:35
  34.2 3.6 %all-to-all-start.1 = ((bf16[2,2,88,352]{3,2,1,0:T(8,128)(2,1)}), bf16[2,2,88,352]{3,2,1,0:T(8,128)(2,1)S(1)}, u32[]{:S(2)}, u32[]{:S(2)}) async-start(bf16[2,2,88,352]{3,2,1,0:T(8,128)(2,1)} %bitcast.1), calls=%async_computation.1 | async-start | bytes 540672 | tf_op jit(solution)/shard_map/all_to_all | solution.py:42
  37.8 0.3 convolution_reduce_fusion.1
  38.1 0.1 bitcast_reduce_fusion.2
  38.3 5.2 %all-to-all-done.1 = bf16[2,2,88,352]{3,2,1,0:T(8,128)(2,1)S(1)} async-done(((bf16[2,2,88,352]{3,2,1,0:T(8,128)(2,1)}), bf16[2,2,88,352]{3,2,1,0:T(8,128)(2,1)S(1)}, u32[]{:S(2)}, u32[]{:S(2)}) %all-to-all-start.1) | async-done | bytes 247840 | tf_op jit(solution)/shard_map/all_to_all | solution.py:42
  43.5 3.4 %all-to-all-start.4 = ((bf16[2,2,88,352]{3,2,1,0:T(8,128)(2,1)}), bf16[2,2,88,352]{3,2,1,0:T(8,128)(2,1)S(1)}, u32[]{:S(2)}, u32[]{:S(2)}) async-start(bf16[2,2,88,352]{3,2,1,0:T(8,128)(2,1)} %bitcast.8), calls=%async_computation.4 | async-start | bytes 540672 | tf_op jit(solution)/shard_map/all_to_all | solution.py:42
  47.0 5.2 %all-to-all-done.4 = bf16[2,2,88,352]{3,2,1,0:T(8,128)(2,1)S(1)} async-done(((bf16[2,2,88,352]{3,2,1,0:T(8,128)(2,1)}), bf16[2,2,88,352]{3,2,1,0:T(8,128)(2,1)S(1)}, u32[]{:S(2)}, u32[]{:S(2)}) %all-to-all-start.4) | async-done | bytes 247840 | tf_op jit(solution)/shard_map/all_to_all | solution.py:42
  52.1 3.4 %all-to-all-start.7 = ((bf16[2,2,88,352]{3,2,1,0:T(8,128)(2,1)}), bf16[2,2,88,352]{3,2,1,0:T(8,128)(2,1)S(1)}, u32[]{:S(2)}, u32[]{:S(2)}) async-start(bf16[2,2,88,352]{3,2,1,0:T(8,128)(2,1)} %bitcast.15), calls=%async_computation.7 | async-start | bytes 540672 | tf_op jit(solution)/shard_map/all_to_all | solution.py:42
  55.6 0.1 broadcast_multiply_fusion.1
  55.6 0.7 copy.34
  56.4 4.4 %all-to-all-done.7 = bf16[2,2,88,352]{3,2,1,0:T(8,128)(2,1)S(1)} async-done(((bf16[2,2,88,352]{3,2,1,0:T(8,128)(2,1)}), bf16[2,2,88,352]{3,2,1,0:T(8,128)(2,1)S(1)}, u32[]{:S(2)}, u32[]{:S(2)}) %all-to-all-start.7) | async-done | bytes 247840 | tf_op jit(solution)/shard_map/all_to_all | solution.py:42
  60.8 5.1 %all-to-all-start.2 = ((bf16[4,1,1,88,352]{4,3,2,1,0:T(8,128)(2,1)}), bf16[4,1,1,88,352]{4,3,2,1,0:T(8,128)(2,1)S(1)}, u32[]{:S(2)}, u32[]{:S(2)}) async-start(bf16[4,1,1,88,352]{4,3,2,1,0:T(8,128)(2,1)} %bitcast.5), calls=%async_computation.2 | async-start | bytes 540672 | tf_op jit(solution)/shard_map/all_to_all | solution.py:50
  65.9 0.1 broadcast_multiply_fusion
  65.9 39.9 %psum.7 = f32[3,2,4,11]{3,2,1,0:T(4,128)S(1)} all-reduce(f32[3,2,4,11]{3,2,1,0:T(4,128)S(1)} %broadcast_multiply_fusion), channel_id=1, replica_groups=mesh['dp'=4,'pipe'=2,'tensor'=4] {'dp','pipe','tensor'}, use_global_device_ids=true, to_apply=%region_3.4 | all-reduce | flops 264 | bytes 2112 | tf_op jit(solution)/shard_map/psum | solution.py:77
  105.8 0.6 dynamic-slice_multiply_fusion
  106.4 0.7 copy.38
  107.1 0.7 copy.42
  107.9 0.0 all-to-all-done.2
  107.9 3.6 %all-to-all-start.5 = ((bf16[4,1,1,88,352]{4,3,2,1,0:T(8,128)(2,1)}), bf16[4,1,1,88,352]{4,3,2,1,0:T(8,128)(2,1)S(1)}, u32[]{:S(2)}, u32[]{:S(2)}) async-start(bf16[4,1,1,88,352]{4,3,2,1,0:T(8,128)(2,1)} %bitcast.12), calls=%async_computation.5 | async-start | bytes 540672 | tf_op jit(solution)/shard_map/all_to_all | solution.py:50
  111.4 0.2 copy.36
  111.6 11.0 %all_gather.9 = bf16[352,1408]{0,1:T(8,128)(2,1)S(1)} all-gather(bf16[352,352]{0,1:T(8,128)(2,1)S(1)} %copy.36), channel_id=1, replica_groups=mesh['dp'=4,'pipe'=2,'tensor'=4] {'dp'}, dimensions={1}, use_global_device_ids=true | all-gather | bytes 1239040 | tf_op jit(solution)/shard_map/all_gather | solution.py:56
  122.6 1.9 %copy.45 = bf16[352,1408]{1,0:T(8,128)(2,1)} copy(bf16[352,1408]{0,1:T(8,128)(2,1)S(1)} %all_gather.9) | data formatting | bytes 1982464
  124.5 0.0 all-to-all-done.5
  124.5 5.1 %all-to-all-start.8 = ((bf16[4,1,1,88,352]{4,3,2,1,0:T(8,128)(2,1)}), bf16[4,1,1,88,352]{4,3,2,1,0:T(8,128)(2,1)S(1)}, u32[]{:S(2)}, u32[]{:S(2)}) async-start(bf16[4,1,1,88,352]{4,3,2,1,0:T(8,128)(2,1)} %bitcast.19), calls=%async_computation.8 | async-start | bytes 540672 | tf_op jit(solution)/shard_map/all_to_all | solution.py:50
  129.6 0.2 copy.40
  129.8 10.0 %all_gather.10 = bf16[352,1408]{0,1:T(8,128)(2,1)S(1)} all-gather(bf16[352,352]{0,1:T(8,128)(2,1)S(1)} %copy.40), channel_id=1, replica_groups=mesh['dp'=4,'pipe'=2,'tensor'=4] {'dp'}, dimensions={1}, use_global_device_ids=true | all-gather | bytes 1239040 | tf_op jit(solution)/shard_map/all_gather | solution.py:56
  139.8 1.9 %copy.46 = bf16[352,1408]{1,0:T(8,128)(2,1)} copy(bf16[352,1408]{0,1:T(8,128)(2,1)S(1)} %all_gather.10) | data formatting | bytes 1982464
  141.7 0.0 all-to-all-done.8
  141.7 0.2 copy.44
  141.9 10.3 %all_gather.11 = bf16[352,1408]{0,1:T(8,128)(2,1)S(1)} all-gather(bf16[352,352]{0,1:T(8,128)(2,1)S(1)} %copy.44), channel_id=1, replica_groups=mesh['dp'=4,'pipe'=2,'tensor'=4] {'dp'}, dimensions={1}, use_global_device_ids=true | all-gather | bytes 1239040 | tf_op jit(solution)/shard_map/all_gather | solution.py:56
  152.2 1.9 %copy.47 = bf16[352,1408]{1,0:T(8,128)(2,1)} copy(bf16[352,1408]{0,1:T(8,128)(2,1)S(1)} %all_gather.11) | data formatting | bytes 1982464
  (9 shorter events, 0.0 us)
Async XLA Ops:
  0.6 27.4 %copy-start = (f32[1408]{0:T(1024)S(1)}, f32[1408]{0:T(1024)}, u32[]{:S(2)}) copy-start(f32[1408]{0:T(1024)} %param.8) | copy-start | bytes 16900
  0.6 6.4 %copy-start.3 = (bf16[88,1408]{1,0:T(8,128)(2,1)S(1)}, bf16[88,1408]{1,0:T(8,128)(2,1)}, u32[]{:S(2)}) copy-start(bf16[88,1408]{1,0:T(8,128)(2,1)} %param.6) | copy-start | bytes 743428
  2.7 15.2 %copy-start.2 = (bf16[88,1408]{1,0:T(8,128)(2,1)S(1)}, bf16[88,1408]{1,0:T(8,128)(2,1)}, u32[]{:S(2)}) copy-start(bf16[88,1408]{1,0:T(8,128)(2,1)} %param.7) | copy-start | bytes 743428
  2.7 11.0 %all-to-all-start = ((bf16[88,4,352]{2,0,1:T(8,128)(2,1)}), bf16[88,4,352]{2,0,1:T(8,128)(2,1)}, u32[]{:S(2)}, u32[]{:S(2)}) async-start(bf16[88,4,352]{2,0,1:T(8,128)(2,1)} %copy.33), calls=%async_computation | async-start | bytes 540672 | tf_op jit(solution)/shard_map/all_to_all | solution.py:33
  8.1 20.0 %copy-start.1 = (bf16[88,1408]{1,0:T(8,128)(2,1)S(1)}, bf16[88,1408]{1,0:T(8,128)(2,1)}, u32[]{:S(2)}) copy-start(bf16[88,1408]{1,0:T(8,128)(2,1)} %param.5) | copy-start | bytes 743428
  13.7 10.2 %all-to-all-start.3 = ((bf16[88,4,352]{2,0,1:T(8,128)(2,1)}), bf16[88,4,352]{2,0,1:T(8,128)(2,1)}, u32[]{:S(2)}, u32[]{:S(2)}) async-start(bf16[88,4,352]{2,0,1:T(8,128)(2,1)} %copy.37), calls=%async_computation.3 | async-start | bytes 540672 | tf_op jit(solution)/shard_map/all_to_all | solution.py:34
  18.1 20.0 %copy-start.4 = (f32[1408]{0:T(1024)S(1)}, f32[1408]{0:T(1024)}, u32[]{:S(2)}) copy-start(f32[1408]{0:T(1024)} %param.9) | copy-start | bytes 16900
  24.0 10.2 %all-to-all-start.6 = ((bf16[88,4,352]{2,0,1:T(8,128)(2,1)}), bf16[88,4,352]{2,0,1:T(8,128)(2,1)}, u32[]{:S(2)}, u32[]{:S(2)}) async-start(bf16[88,4,352]{2,0,1:T(8,128)(2,1)} %copy.41), calls=%async_computation.6 | async-start | bytes 540672 | tf_op jit(solution)/shard_map/all_to_all | solution.py:35
  34.2 9.3 %all-to-all-start.1 = ((bf16[2,2,88,352]{3,2,1,0:T(8,128)(2,1)}), bf16[2,2,88,352]{3,2,1,0:T(8,128)(2,1)S(1)}, u32[]{:S(2)}, u32[]{:S(2)}) async-start(bf16[2,2,88,352]{3,2,1,0:T(8,128)(2,1)} %bitcast.1), calls=%async_computation.1 | async-start | bytes 540672 | tf_op jit(solution)/shard_map/all_to_all | solution.py:42
  43.5 8.7 %all-to-all-start.4 = ((bf16[2,2,88,352]{3,2,1,0:T(8,128)(2,1)}), bf16[2,2,88,352]{3,2,1,0:T(8,128)(2,1)S(1)}, u32[]{:S(2)}, u32[]{:S(2)}) async-start(bf16[2,2,88,352]{3,2,1,0:T(8,128)(2,1)} %bitcast.8), calls=%async_computation.4 | async-start | bytes 540672 | tf_op jit(solution)/shard_map/all_to_all | solution.py:42
  52.1 8.7 %all-to-all-start.7 = ((bf16[2,2,88,352]{3,2,1,0:T(8,128)(2,1)}), bf16[2,2,88,352]{3,2,1,0:T(8,128)(2,1)S(1)}, u32[]{:S(2)}, u32[]{:S(2)}) async-start(bf16[2,2,88,352]{3,2,1,0:T(8,128)(2,1)} %bitcast.15), calls=%async_computation.7 | async-start | bytes 540672 | tf_op jit(solution)/shard_map/all_to_all | solution.py:42
  60.8 47.1 %all-to-all-start.2 = ((bf16[4,1,1,88,352]{4,3,2,1,0:T(8,128)(2,1)}), bf16[4,1,1,88,352]{4,3,2,1,0:T(8,128)(2,1)S(1)}, u32[]{:S(2)}, u32[]{:S(2)}) async-start(bf16[4,1,1,88,352]{4,3,2,1,0:T(8,128)(2,1)} %bitcast.5), calls=%async_computation.2 | async-start | bytes 540672 | tf_op jit(solution)/shard_map/all_to_all | solution.py:50
  107.9 16.6 %all-to-all-start.5 = ((bf16[4,1,1,88,352]{4,3,2,1,0:T(8,128)(2,1)}), bf16[4,1,1,88,352]{4,3,2,1,0:T(8,128)(2,1)S(1)}, u32[]{:S(2)}, u32[]{:S(2)}) async-start(bf16[4,1,1,88,352]{4,3,2,1,0:T(8,128)(2,1)} %bitcast.12), calls=%async_computation.5 | async-start | bytes 540672 | tf_op jit(solution)/shard_map/all_to_all | solution.py:50
  124.5 17.2 %all-to-all-start.8 = ((bf16[4,1,1,88,352]{4,3,2,1,0:T(8,128)(2,1)}), bf16[4,1,1,88,352]{4,3,2,1,0:T(8,128)(2,1)S(1)}, u32[]{:S(2)}, u32[]{:S(2)}) async-start(bf16[4,1,1,88,352]{4,3,2,1,0:T(8,128)(2,1)} %bitcast.19), calls=%async_computation.8 | async-start | bytes 540672 | tf_op jit(solution)/shard_map/all_to_all | solution.py:50
where the time goes:
time: 155 us; the launch traced here: 154 us
  blocking collectives  71.2 us (46%)
  starting transfers between devices  36.7 us (24%)
  waiting for transfers between devices  31 us (20%)
  local copies, waits for them, and re-layouts  12.5 us (8%)
    psum x1, blocking collectives, shards(): summed = lax.psum(spread, ('dp', 'pipe', 'tensor'))  39.9 us
    all_gather x3, blocking collectives, shards(): lax.all_gather(for_sending(flat_pieces), 'dp', axis=1, tiled=True)  31.3 us
    all_to_all x3, waiting for transfers between devices, shards(): lax.all_to_all(for_sending(grouped), 'pipe', split_axis=0, concat_axis=2,...  14.7 us
    all_to_all x3, starting transfers between devices, shards(): lax.all_to_all(for_sending(routed), 'tensor', split_axis=0, concat_axis=2...  13.7 us
    all_to_all x3, starting transfers between devices, shards(): lax.all_to_all(for_sending(grouped), 'pipe', split_axis=0, concat_axis=2,...  10.5 us
    unnamed x13, local copies, waits for them, and re-layouts  5.65 us
    all_to_all x1, waiting for transfers between devices, shards(): lax.all_to_all(sources[0], 'dp', split_axis=1, concat_axis=0, tiled=True)  5.65 us
    all_to_all x1, waiting for transfers between devices, shards(): lax.all_to_all(sources[2], 'dp', split_axis=1, concat_axis=0, tiled=True)  5.51 us
  transfers between devices with their start and end apart: 9, of which 6 were waited for; matrix products, arithmetic and copies ran while one was open for 6% of the time, Pallas kernels for 0%

commit v1 on v0

--- a/solution.py
+++ b/solution.py
@@ -74,7 +74,8 @@
         * section_hit[None, :, None, None]
         * tile_hit[None, None, :, None]
     )
-    summed = lax.psum(spread, ("dp", "pipe", "tensor"))
+    blocks = lax.all_gather(spread, ("dp", "pipe", "tensor"), axis=0, tiled=False)
+    summed = blocks.sum(axis=0)
     checks = (
         lax.dynamic_slice(summed, (0, lax.axis_index("pipe"), tensor_pos, 0), (3, 1, 1, col_blocks))
         * factor

time: 155 us -> 183 us (1.18)
  blocking collectives: 71.2 us -> 98.8 us
    all_gather x0 -> x1, blocking collectives: none -> 68.7 us  [shards(): lax.all_gather(spread, ('dp', 'pipe', 'tensor'), axis=0, tiled=False)]
    psum x1 -> x0, blocking collectives: 39.9 us -> none  [shards(): summed = lax.psum(spread, ('dp', 'pipe', 'tensor'))]
  transfers between devices with their start and end apart: 9 -> 9, of which waited for: 6 -> 6; matrix products, arithmetic and copies ran while one was open for 6% -> 5% of each run, Pallas kernels for 0% -> 0%
where the time goes in v1:
time: 183 us; the launch traced here: 182 us
  blocking collectives  98.8 us (54%)
  starting transfers between devices  36.6 us (20%)
  waiting for transfers between devices  31 us (17%)
  local copies, waits for them, and re-layouts  12.5 us (7%)
    all_gather x1, blocking collectives, shards(): lax.all_gather(spread, ('dp', 'pipe', 'tensor'), axis=0, tiled=False)  68.7 us
    all_gather x3, blocking collectives, shards(): lax.all_gather(for_sending(flat_pieces), 'dp', axis=1, tiled=True)  30.1 us
    all_to_all x3, waiting for transfers between devices, shards(): lax.all_to_all(for_sending(grouped), 'pipe', split_axis=0, concat_axis=2,...  14.7 us
    all_to_all x3, starting transfers between devices, shards(): lax.all_to_all(for_sending(routed), 'tensor', split_axis=0, concat_axis=2...  13.6 us
    all_to_all x3, starting transfers between devices, shards(): lax.all_to_all(for_sending(grouped), 'pipe', split_axis=0, concat_axis=2,...  10.5 us
    unnamed x13, local copies, waits for them, and re-layouts  5.65 us
    all_to_all x1, waiting for transfers between devices, shards(): lax.all_to_all(sources[0], 'dp', split_axis=1, concat_axis=0, tiled=True)  5.65 us
    all_to_all x1, waiting for transfers between devices, shards(): lax.all_to_all(sources[2], 'dp', split_axis=1, concat_axis=0, tiled=True)  5.51 us
  transfers between devices with their start and end apart: 9, of which 6 were waited for; matrix products, arithmetic and copies ran while one was open for 5% of the time, Pallas kernels for 0%

profile of v1, /device:TPU:0, one launch (start us, length us, event | category | flops | bytes accessed | tf_op | source)
XLA Modules:
  0.0 181.7 jit_solution(5992815658888185025)
XLA Ops:
  0.6 0.0 copy-start
  0.6 0.0 copy-start.3
  0.7 1.3 all_to_all.90
  1.9 0.7 copy.33
  2.7 4.4 %all-to-all-start = ((bf16[88,4,352]{2,0,1:T(8,128)(2,1)}), bf16[88,4,352]{2,0,1:T(8,128)(2,1)}, u32[]{:S(2)}, u32[]{:S(2)}) async-start(bf16[88,4,352]{2,0,1:T(8,128)(2,1)} %copy.33), calls=%async_computation | async-start | bytes 540672 | tf_op jit(solution)/shard_map/all_to_all | solution.py:33
  7.0 0.3 all_to_all.97
  7.3 0.7 copy.37
  8.1 5.6 %all-to-all-done = bf16[88,4,352]{2,0,1:T(8,128)(2,1)} async-done(((bf16[88,4,352]{2,0,1:T(8,128)(2,1)}), bf16[88,4,352]{2,0,1:T(8,128)(2,1)}, u32[]{:S(2)}, u32[]{:S(2)}) %all-to-all-start) | async-done | bytes 247840 | tf_op jit(solution)/shard_map/all_to_all | solution.py:33
  13.7 4.1 %all-to-all-start.3 = ((bf16[88,4,352]{2,0,1:T(8,128)(2,1)}), bf16[88,4,352]{2,0,1:T(8,128)(2,1)}, u32[]{:S(2)}, u32[]{:S(2)}) async-start(bf16[88,4,352]{2,0,1:T(8,128)(2,1)} %copy.37), calls=%async_computation.3 | async-start | bytes 540672 | tf_op jit(solution)/shard_map/all_to_all | solution.py:34
  17.8 0.3 all_to_all.104
  18.1 0.0 copy-start.4
  18.1 0.7 copy.41
  18.9 5.1 %all-to-all-done.3 = bf16[88,4,352]{2,0,1:T(8,128)(2,1)} async-done(((bf16[88,4,352]{2,0,1:T(8,128)(2,1)}), bf16[88,4,352]{2,0,1:T(8,128)(2,1)}, u32[]{:S(2)}, u32[]{:S(2)}) %all-to-all-start.3) | async-done | bytes 247840 | tf_op jit(solution)/shard_map/all_to_all | solution.py:34
  24.0 4.1 %all-to-all-start.6 = ((bf16[88,4,352]{2,0,1:T(8,128)(2,1)}), bf16[88,4,352]{2,0,1:T(8,128)(2,1)}, u32[]{:S(2)}, u32[]{:S(2)}) async-start(bf16[88,4,352]{2,0,1:T(8,128)(2,1)} %copy.41), calls=%async_computation.6 | async-start | bytes 540672 | tf_op jit(solution)/shard_map/all_to_all | solution.py:35
  28.1 0.3 convolution_reduce_fusion.2
  28.4 0.3 convolution_reduce_fusion
  28.7 5.5 %all-to-all-done.6 = bf16[88,4,352]{2,0,1:T(8,128)(2,1)} async-done(((bf16[88,4,352]{2,0,1:T(8,128)(2,1)}), bf16[88,4,352]{2,0,1:T(8,128)(2,1)}, u32[]{:S(2)}, u32[]{:S(2)}) %all-to-all-start.6) | async-done | bytes 247840 | tf_op jit(solution)/shard_map/all_to_all | solution.py:35
  34.2 3.6 %all-to-all-start.1 = ((bf16[2,2,88,352]{3,2,1,0:T(8,128)(2,1)}), bf16[2,2,88,352]{3,2,1,0:T(8,128)(2,1)S(1)}, u32[]{:S(2)}, u32[]{:S(2)}) async-start(bf16[2,2,88,352]{3,2,1,0:T(8,128)(2,1)} %bitcast.1), calls=%async_computation.1 | async-start | bytes 540672 | tf_op jit(solution)/shard_map/all_to_all | solution.py:42
  37.8 0.3 convolution_reduce_fusion.1
  38.1 0.1 bitcast_reduce_fusion.2
  38.3 5.2 %all-to-all-done.1 = bf16[2,2,88,352]{3,2,1,0:T(8,128)(2,1)S(1)} async-done(((bf16[2,2,88,352]{3,2,1,0:T(8,128)(2,1)}), bf16[2,2,88,352]{3,2,1,0:T(8,128)(2,1)S(1)}, u32[]{:S(2)}, u32[]{:S(2)}) %all-to-all-start.1) | async-done | bytes 247840 | tf_op jit(solution)/shard_map/all_to_all | solution.py:42
  43.5 3.4 %all-to-all-start.4 = ((bf16[2,2,88,352]{3,2,1,0:T(8,128)(2,1)}), bf16[2,2,88,352]{3,2,1,0:T(8,128)(2,1)S(1)}, u32[]{:S(2)}, u32[]{:S(2)}) async-start(bf16[2,2,88,352]{3,2,1,0:T(8,128)(2,1)} %bitcast.8), calls=%async_computation.4 | async-start | bytes 540672 | tf_op jit(solution)/shard_map/all_to_all | solution.py:42
  47.0 5.2 %all-to-all-done.4 = bf16[2,2,88,352]{3,2,1,0:T(8,128)(2,1)S(1)} async-done(((bf16[2,2,88,352]{3,2,1,0:T(8,128)(2,1)}), bf16[2,2,88,352]{3,2,1,0:T(8,128)(2,1)S(1)}, u32[]{:S(2)}, u32[]{:S(2)}) %all-to-all-start.4) | async-done | bytes 247840 | tf_op jit(solution)/shard_map/all_to_all | solution.py:42
  52.1 3.4 %all-to-all-start.7 = ((bf16[2,2,88,352]{3,2,1,0:T(8,128)(2,1)}), bf16[2,2,88,352]{3,2,1,0:T(8,128)(2,1)S(1)}, u32[]{:S(2)}, u32[]{:S(2)}) async-start(bf16[2,2,88,352]{3,2,1,0:T(8,128)(2,1)} %bitcast.15), calls=%async_computation.7 | async-start | bytes 540672 | tf_op jit(solution)/shard_map/all_to_all | solution.py:42
  55.6 0.1 broadcast_multiply_fusion.1
  55.6 0.7 copy.34
  56.4 4.4 %all-to-all-done.7 = bf16[2,2,88,352]{3,2,1,0:T(8,128)(2,1)S(1)} async-done(((bf16[2,2,88,352]{3,2,1,0:T(8,128)(2,1)}), bf16[2,2,88,352]{3,2,1,0:T(8,128)(2,1)S(1)}, u32[]{:S(2)}, u32[]{:S(2)}) %all-to-all-start.7) | async-done | bytes 247840 | tf_op jit(solution)/shard_map/all_to_all | solution.py:42
  60.8 5.1 %all-to-all-start.2 = ((bf16[4,1,1,88,352]{4,3,2,1,0:T(8,128)(2,1)}), bf16[4,1,1,88,352]{4,3,2,1,0:T(8,128)(2,1)S(1)}, u32[]{:S(2)}, u32[]{:S(2)}) async-start(bf16[4,1,1,88,352]{4,3,2,1,0:T(8,128)(2,1)} %bitcast.5), calls=%async_computation.2 | async-start | bytes 540672 | tf_op jit(solution)/shard_map/all_to_all | solution.py:50
  65.9 0.1 broadcast_multiply_fusion
  65.9 68.7 %all_gather.16 = f32[32,3,2,4,11]{4,3,2,1,0:T(4,128)S(1)} all-gather(f32[1,3,2,4,11]{4,3,2,1,0:T(4,128)S(1)} %broadcast_multiply_fusion), channel_id=1, replica_groups=mesh['dp'=4,'pipe'=2,'tensor'=4] {'dp','pipe','tensor'}, dimensions={0}, use_global_device_ids=true | all-gather | bytes 34848 | tf_op jit(solution)/shard_map/all_gather | solution.py:77
  134.7 0.1 reduce_sum.39
  134.8 0.6 dynamic-slice_multiply_fusion
  135.3 0.7 copy.38
  136.1 0.7 copy.42
  136.8 0.0 all-to-all-done.2
  136.8 3.5 %all-to-all-start.5 = ((bf16[4,1,1,88,352]{4,3,2,1,0:T(8,128)(2,1)}), bf16[4,1,1,88,352]{4,3,2,1,0:T(8,128)(2,1)S(1)}, u32[]{:S(2)}, u32[]{:S(2)}) async-start(bf16[4,1,1,88,352]{4,3,2,1,0:T(8,128)(2,1)} %bitcast.12), calls=%async_computation.5 | async-start | bytes 540672 | tf_op jit(solution)/shard_map/all_to_all | solution.py:50
  140.3 0.2 copy.36
  140.5 9.8 %all_gather.13 = bf16[352,1408]{0,1:T(8,128)(2,1)S(1)} all-gather(bf16[352,352]{0,1:T(8,128)(2,1)S(1)} %copy.36), channel_id=1, replica_groups=mesh['dp'=4,'pipe'=2,'tensor'=4] {'dp'}, dimensions={1}, use_global_device_ids=true | all-gather | bytes 1239040 | tf_op jit(solution)/shard_map/all_gather | solution.py:56
  150.2 1.9 %copy.45 = bf16[352,1408]{1,0:T(8,128)(2,1)} copy(bf16[352,1408]{0,1:T(8,128)(2,1)S(1)} %all_gather.13) | data formatting | bytes 1982464
  152.1 0.0 all-to-all-done.5
  152.1 5.1 %all-to-all-start.8 = ((bf16[4,1,1,88,352]{4,3,2,1,0:T(8,128)(2,1)}), bf16[4,1,1,88,352]{4,3,2,1,0:T(8,128)(2,1)S(1)}, u32[]{:S(2)}, u32[]{:S(2)}) async-start(bf16[4,1,1,88,352]{4,3,2,1,0:T(8,128)(2,1)} %bitcast.19), calls=%async_computation.8 | async-start | bytes 540672 | tf_op jit(solution)/shard_map/all_to_all | solution.py:50
  157.2 0.2 copy.40
  157.4 10.0 %all_gather.14 = bf16[352,1408]{0,1:T(8,128)(2,1)S(1)} all-gather(bf16[352,352]{0,1:T(8,128)(2,1)S(1)} %copy.40), channel_id=1, replica_groups=mesh['dp'=4,'pipe'=2,'tensor'=4] {'dp'}, dimensions={1}, use_global_device_ids=true | all-gather | bytes 1239040 | tf_op jit(solution)/shard_map/all_gather | solution.py:56
  167.4 1.9 %copy.46 = bf16[352,1408]{1,0:T(8,128)(2,1)} copy(bf16[352,1408]{0,1:T(8,128)(2,1)S(1)} %all_gather.14) | data formatting | bytes 1982464
  169.3 0.0 all-to-all-done.8
  169.3 0.2 copy.44
  169.5 10.3 %all_gather.15 = bf16[352,1408]{0,1:T(8,128)(2,1)S(1)} all-gather(bf16[352,352]{0,1:T(8,128)(2,1)S(1)} %copy.44), channel_id=1, replica_groups=mesh['dp'=4,'pipe'=2,'tensor'=4] {'dp'}, dimensions={1}, use_global_device_ids=true | all-gather | bytes 1239040 | tf_op jit(solution)/shard_map/all_gather | solution.py:56
  179.8 1.9 %copy.47 = bf16[352,1408]{1,0:T(8,128)(2,1)} copy(bf16[352,1408]{0,1:T(8,128)(2,1)S(1)} %all_gather.15) | data formatting | bytes 1982464
  (10 shorter events, 0.0 us)
Async XLA Ops:
  0.6 27.4 %copy-start = (f32[1408]{0:T(1024)S(1)}, f32[1408]{0:T(1024)}, u32[]{:S(2)}) copy-start(f32[1408]{0:T(1024)} %param.8) | copy-start | bytes 16900
  0.6 6.4 %copy-start.3 = (bf16[88,1408]{1,0:T(8,128)(2,1)S(1)}, bf16[88,1408]{1,0:T(8,128)(2,1)}, u32[]{:S(2)}) copy-start(bf16[88,1408]{1,0:T(8,128)(2,1)} %param.6) | copy-start | bytes 743428
  2.7 15.2 %copy-start.2 = (bf16[88,1408]{1,0:T(8,128)(2,1)S(1)}, bf16[88,1408]{1,0:T(8,128)(2,1)}, u32[]{:S(2)}) copy-start(bf16[88,1408]{1,0:T(8,128)(2,1)} %param.7) | copy-start | bytes 743428
  2.7 11.0 %all-to-all-start = ((bf16[88,4,352]{2,0,1:T(8,128)(2,1)}), bf16[88,4,352]{2,0,1:T(8,128)(2,1)}, u32[]{:S(2)}, u32[]{:S(2)}) async-start(bf16[88,4,352]{2,0,1:T(8,128)(2,1)} %copy.33), calls=%async_computation | async-start | bytes 540672 | tf_op jit(solution)/shard_map/all_to_all | solution.py:33
  8.1 20.0 %copy-start.1 = (bf16[88,1408]{1,0:T(8,128)(2,1)S(1)}, bf16[88,1408]{1,0:T(8,128)(2,1)}, u32[]{:S(2)}) copy-start(bf16[88,1408]{1,0:T(8,128)(2,1)} %param.5) | copy-start | bytes 743428
  13.7 10.2 %all-to-all-start.3 = ((bf16[88,4,352]{2,0,1:T(8,128)(2,1)}), bf16[88,4,352]{2,0,1:T(8,128)(2,1)}, u32[]{:S(2)}, u32[]{:S(2)}) async-start(bf16[88,4,352]{2,0,1:T(8,128)(2,1)} %copy.37), calls=%async_computation.3 | async-start | bytes 540672 | tf_op jit(solution)/shard_map/all_to_all | solution.py:34
  18.1 20.0 %copy-start.4 = (f32[1408]{0:T(1024)S(1)}, f32[1408]{0:T(1024)}, u32[]{:S(2)}) copy-start(f32[1408]{0:T(1024)} %param.9) | copy-start | bytes 16900
  24.0 10.2 %all-to-all-start.6 = ((bf16[88,4,352]{2,0,1:T(8,128)(2,1)}), bf16[88,4,352]{2,0,1:T(8,128)(2,1)}, u32[]{:S(2)}, u32[]{:S(2)}) async-start(bf16[88,4,352]{2,0,1:T(8,128)(2,1)} %copy.41), calls=%async_computation.6 | async-start | bytes 540672 | tf_op jit(solution)/shard_map/all_to_all | solution.py:35
  34.2 9.3 %all-to-all-start.1 = ((bf16[2,2,88,352]{3,2,1,0:T(8,128)(2,1)}), bf16[2,2,88,352]{3,2,1,0:T(8,128)(2,1)S(1)}, u32[]{:S(2)}, u32[]{:S(2)}) async-start(bf16[2,2,88,352]{3,2,1,0:T(8,128)(2,1)} %bitcast.1), calls=%async_computation.1 | async-start | bytes 540672 | tf_op jit(solution)/shard_map/all_to_all | solution.py:42
  43.5 8.7 %all-to-all-start.4 = ((bf16[2,2,88,352]{3,2,1,0:T(8,128)(2,1)}), bf16[2,2,88,352]{3,2,1,0:T(8,128)(2,1)S(1)}, u32[]{:S(2)}, u32[]{:S(2)}) async-start(bf16[2,2,88,352]{3,2,1,0:T(8,128)(2,1)} %bitcast.8), calls=%async_computation.4 | async-start | bytes 540672 | tf_op jit(solution)/shard_map/all_to_all | solution.py:42
  52.1 8.7 %all-to-all-start.7 = ((bf16[2,2,88,352]{3,2,1,0:T(8,128)(2,1)}), bf16[2,2,88,352]{3,2,1,0:T(8,128)(2,1)S(1)}, u32[]{:S(2)}, u32[]{:S(2)}) async-start(bf16[2,2,88,352]{3,2,1,0:T(8,128)(2,1)} %bitcast.15), calls=%async_computation.7 | async-start | bytes 540672 | tf_op jit(solution)/shard_map/all_to_all | solution.py:42
  60.8 76.0 %all-to-all-start.2 = ((bf16[4,1,1,88,352]{4,3,2,1,0:T(8,128)(2,1)}), bf16[4,1,1,88,352]{4,3,2,1,0:T(8,128)(2,1)S(1)}, u32[]{:S(2)}, u32[]{:S(2)}) async-start(bf16[4,1,1,88,352]{4,3,2,1,0:T(8,128)(2,1)} %bitcast.5), calls=%async_computation.2 | async-start | bytes 540672 | tf_op jit(solution)/shard_map/all_to_all | solution.py:50
  136.8 15.3 %all-to-all-start.5 = ((bf16[4,1,1,88,352]{4,3,2,1,0:T(8,128)(2,1)}), bf16[4,1,1,88,352]{4,3,2,1,0:T(8,128)(2,1)S(1)}, u32[]{:S(2)}, u32[]{:S(2)}) async-start(bf16[4,1,1,88,352]{4,3,2,1,0:T(8,128)(2,1)} %bitcast.12), calls=%async_computation.5 | async-start | bytes 540672 | tf_op jit(solution)/shard_map/all_to_all | solution.py:50
  152.1 17.2 %all-to-all-start.8 = ((bf16[4,1,1,88,352]{4,3,2,1,0:T(8,128)(2,1)}), bf16[4,1,1,88,352]{4,3,2,1,0:T(8,128)(2,1)S(1)}, u32[]{:S(2)}, u32[]{:S(2)}) async-start(bf16[4,1,1,88,352]{4,3,2,1,0:T(8,128)(2,1)} %bitcast.19), calls=%async_computation.8 | async-start | bytes 540672 | tf_op jit(solution)/shard_map/all_to_all | solution.py:50
